TPU v7x, 32 devices: a whole 2x2x4 slice. The times are simulated.
32 devices in a mesh: col: 8 (over y, x, core), row: 4 (over z).
Axes of the slice: x: 2, y: 2, z: 4, core: 2. Of those that a mesh axis runs over, the one named last changes fastest.
Arguments:
- visibilities: bfloat16 [2, 8192, 4096], P(None, 'col', 'row'), may hold values from -6 to 6
- col_offsets: int32 [8], P('col'), may hold values from 0 to 15360
- row_offsets: int32 [4], replicated, may hold values from 0 to 15360
- facet_offsets: int32 [8, 2], replicated, may hold values from 0 to 16383
- facet_order: int32 [8], replicated, may hold values from 0 to 7, each once
- vis_counts: int32 [8, 4], P('col', 'row'), may hold values from 512 to 1024
Outputs:
- facet_images: float32 [8, 2, 64, 4096], P('col', None, None, 'row')
- peak: float32 [8], P('col')
Inputs may be any that keep to these rules, and one draw needn't show every extreme that they name: `facet_order`: each slot names a different facet.
All inputs are finite; a program needn't handle non-finite values.
Results may differ from a plain program's by a relative error of at most 0.0078.
Values may be sent and summed in bfloat16 or wider, within the bound.
A program may use at most 128 MiB of HBM per device.

v0:
```python
import math

import jax
import jax.numpy as jnp
from jax import lax
from jax.sharding import PartitionSpec as P

M = 1024
FS = 4096
NG = 16384
FR = 64


TWO_PI = 2.0 * math.pi
BEAM_SLOPE = 0.66


def phase_table(first_ids, second_ids, factor):
    product = first_ids[:, None] * second_ids[None, :] % NG
    angles = product.astype(jnp.float32) * (TWO_PI / NG)
    return (
        (jnp.cos(angles) * factor).astype(jnp.bfloat16),
        (jnp.sin(angles) * factor).astype(jnp.bfloat16),
    )


def complex_product(left_real, left_imag, right_real, right_imag):
    left_rows = jnp.concatenate([left_real, left_imag], axis=0)
    right_cols = jnp.concatenate([right_real, right_imag], axis=1)
    product = jnp.dot(left_rows, right_cols, preferred_element_type=jnp.float32)
    product = product.reshape(2, left_real.shape[0], 2, right_real.shape[1])
    real_part = product[0, :, 0] - product[1, :, 1]
    imag_part = product[0, :, 1] + product[1, :, 0]
    return (real_part, imag_part)


def local(visibilities, col_offsets, row_offsets, facet_offsets, facet_order, vis_counts):
    col_count = lax.axis_size("col")
    row_count = lax.axis_size("row")
    col_index = lax.axis_index("col")
    row_index = lax.axis_index("row")
    facets = facet_order.shape[0]
    block_cols = FS // row_count
    slot_pick = (facet_order[:, None] == jnp.arange(facets, dtype=jnp.int32)[None, :]).astype(
        jnp.int32
    )
    slot_offsets = jnp.sum(slot_pick[:, :, None] * facet_offsets[None, :, :], axis=1)
    own_pick = (jnp.arange(facets, dtype=jnp.int32) == col_index).astype(jnp.int32)
    own_facet = jnp.sum(slot_offsets * own_pick[:, None], axis=0)
    row_ids = jnp.arange(M, dtype=jnp.int32)
    live_rows = row_ids < vis_counts[0, 0]
    masked = jnp.where(live_rows[None, :, None], visibilities, jnp.zeros_like(visibilities))
    grid_u = col_offsets[0] + row_ids
    pixel_rows = jnp.arange(FR, dtype=jnp.int32) + (FS // 2 - FR // 2)
    first_scale = 1.0 / math.sqrt(M * col_count)
    second_scale = 0.5 / math.sqrt(M * row_count)
    chosen = slot_offsets[:, 0]
    image_rows = ((chosen[:, None] + pixel_rows[None, :]) % NG).reshape(
        1 * lax.axis_size("col") * FR
    )
    table_real, table_imag = phase_table(image_rows, grid_u, first_scale)
    part_real, part_imag = complex_product(table_real, table_imag, masked[0], masked[1])
    facet_partial = lax.psum_scatter(
        jnp.stack(
            [
                part_real.reshape(1 * lax.axis_size("col"), FR, M),
                part_imag.reshape(1 * lax.axis_size("col"), FR, M),
            ],
            axis=1,
        ),
        "col",
        scatter_dimension=0,
        tiled=True,
    )[0]
    columns = facet_partial.astype(jnp.bfloat16)
    image_cols = (
        own_facet[1] + row_index * block_cols + jnp.arange(block_cols, dtype=jnp.int32)
    ) % NG
    slab_piece = lax.all_gather(columns, "row", axis=2, tiled=True)
    pieces = slab_piece.shape[2] // M
    grid_many = (row_offsets[:, None] + row_ids[None, :]).reshape(pieces * M)
    second_real, second_imag = phase_table(grid_many, image_cols, second_scale)
    out_real, out_imag = complex_product(slab_piece[0], slab_piece[1], second_real, second_imag)
    facet_block = jnp.stack([out_real, out_imag], axis=0)
    beam_cols = (row_index * block_cols + jnp.arange(block_cols, dtype=jnp.int32)).astype(
        jnp.float32
    )
    beam = 1.0 - BEAM_SLOPE * (beam_cols + 0.5) / FS
    facet_images = facet_block / beam[None, None, :]
    magnitude = jnp.sqrt(facet_images[0] * facet_images[0] + facet_images[1] * facet_images[1])
    local_peak = jnp.max(magnitude)
    peak = lax.pmax(local_peak[None], "row")
    return (facet_images[None], peak)


def solution(mesh):
    in_specs = (P(None, "col", "row"), P("col"), P(), P(), P(), P("col", "row"))
    out_specs = (P("col", None, None, "row"), P("col"))
    return jax.shard_map(local, mesh=mesh, in_specs=in_specs, out_specs=out_specs, check_vma=False)
```

profile of v0, /device:TPU:0, one launch (start us, length us, event | category | flops | bytes accessed | tf_op | source)
XLA Modules:
  0.0 214.2 jit_solution(18039350447489056323)
XLA Ops:
  7.2 0.7 fusion.31
  7.9 0.8 multiply_reduce_fusion
  10.3 2.5 %broadcast_select_fusion = bf16[2,1024,1024]{2,1,0:T(8,128)(2,1)S(1)} fusion(bf16[2,1024,1024]{2,1,0:T(8,128)(2,1)} %param.6, pred[1024]{0:T(1024)(128)(4,1)S(1)} %iota_compare_fusion), kind=kLoop, calls=%fused_computation.19 | loop fusion | flops 2097152 | bytes 8389632 | tf_op jit(solution)/shard_map/jit(_where)/select_n | solution.py:52
  12.8 0.4 slice_bitcast_fusion.1
  13.3 9.1 %multiply_convert_fusion.3 = (bf16[512,1024]{1,0:T(8,128)(2,1)S(1)}, bf16[512,1024]{1,0:T(8,128)(2,1)S(1)}) fusion(s32[1024]{0:T(1024)S(1)} %iota_add_fusion, s32[512]{0:T(512)S(1)} %add_select_fusion.3), kind=kLoop, calls=%fused_computation.36 | loop fusion | flops 9437184 | bytes 2103296 | tf_op jit(solution)/shard_map/convert_element_type | solution.py:22
  22.4 6.9 %fusion.7 = f32[1024,2048]{1,0:T(8,128)} fusion(bf16[1024,1024]{1,0:T(8,128)(2,1)S(1)} %get-tuple-element.5, bf16[1024,1024]{1,0:T(8,128)(2,1)S(1)} %get-tuple-element.4, bf16[512,1024]{1,0:T(8,128)(2,1)S(1)} %get-tuple-element.19, bf16[512,1024]{1,0:T(8,128)(2,1)S(1)} %get-tuple-element.18), kind=kOutput, calls=%fused_computation.14 | convolution fusion | flops 4307550208 | bytes 14680064 | tf_op jit(solution)/shard_map/dot_general | solution.py:30
  29.2 11.7 %reshape.233 = f32[2,512,2,1024]{3,2,1,0:T(2,128)} reshape(f32[1024,2048]{1,0:T(8,128)} %fusion.7) | data formatting | bytes 16777216 | tf_op jit(solution)/shard_map/reshape | solution.py:31
  41.0 10.9 %slice_subtract_fusion = (f32[1,512,1,1024]{3,2,1,0:T(1,128)S(1)}, f32[1,512,1,1024]{3,2,1,0:T(1,128)S(1)}) fusion(f32[2,512,2,1024]{3,2,1,0:T(2,128)} %reshape.233), kind=kLoop, calls=%fused_computation.29 | loop fusion | flops 1048576 | bytes 12582912 | tf_op jit(solution)/shard_map/sub | solution.py:32
  51.8 0.5 copy.23
  52.3 0.5 copy.24
  52.8 2.4 %pad_maximum_fusion = f32[8,2,64,1024]{3,2,1,0:T(8,128)} fusion(f32[8,1,64,1024]{3,2,1,0:T(8,128)S(1)} %bitcast.32, f32[8,1,64,1024]{3,2,1,0:T(8,128)S(1)} %bitcast.31), kind=kLoop, calls=%fused_computation.18 | loop fusion | flops 1048576 | bytes 8388608 | tf_op jit(solution)/shard_map/stack | solution.py:64
  55.2 0.2 all-gather.3.cloned.1.call-start
  55.6 0.6 slice.59
  57.0 52.3 %reduce-scatter.2.cloned.1.call-done = f32[1,2,64,1024]{3,2,1,0:T(8,128)} async-done(((f32[8,2,64,1024]{3,2,1,0:T(8,128)}), f32[1,2,64,1024]{3,2,1,0:T(8,128)}) %reduce-scatter.2.cloned.1.call-update) | async-done | bytes 524304 | tf_op jit(solution)/shard_map/reduce_scatter | solution.py:63
  109.3 1.8 convert_element_type.49
  111.1 71.4 %multiply_convert_fusion.1 = (bf16[4096,1024]{1,0:T(8,128)(2,1)}, bf16[4096,1024]{1,0:T(8,128)(2,1)}) fusion(s32[1024]{0:T(1024)S(1)} %add_select_fusion.2, s32[4096]{0:T(1024)S(1)} %bitcast.33), kind=kLoop, calls=%fused_computation.13 | loop fusion | flops 75497472 | bytes 16797696 | tf_op jit(solution)/shard_map/convert_element_type | solution.py:22
  182.5 1.3 slice_bitcast_fusion.3
  183.8 7.8 %fusion.3 = f32[128,2048]{1,0:T(8,128)S(1)} fusion(bf16[4096,1024]{1,0:T(8,128)(2,1)} %get-tuple-element.17, bf16[4096,1024]{1,0:T(8,128)(2,1)} %get-tuple-element.16, bf16[64,4096]{1,0:T(8,128)(2,1)S(1)} %get-tuple-element.11, bf16[64,4096]{1,0:T(8,128)(2,1)S(1)} %get-tuple-element.10), kind=kOutput, calls=%fused_computation.8 | convolution fusion | flops 2183135232 | bytes 18874368 | tf_op jit(solution)/shard_map/dot_general | solution.py:30
  191.5 0.9 reshape.234
  192.4 0.8 fusion.35
  193.2 0.2 fusion.23
  193.5 0.7 fusion.22
  194.2 12.3 %pmax.7 = f32[1]{0:T(128)} all-reduce(f32[1]{0:T(128)} %bitcast.12), channel_id=1, replica_groups=mesh['col'=8,'row'=4] {'row'}, use_global_device_ids=true, to_apply=%region_4.5 | all-reduce | flops 1 | bytes 8 | tf_op jit(solution)/shard_map/pmax | solution.py:92
  206.5 0.9 maximum_divide_fusion
  (20 shorter events, 0.5 us)
Async XLA Ops:
  7.2 102.1 %reduce-scatter.2.cloned.1.call-start = ((), (), s32[]{:S(2)}) async-start(), calls=%async_computation.1 | async-start | bytes 4718592 | tf_op jit(solution)/shard_map/reduce_scatter | solution.py:63
  55.2 1.0 copy-start
  55.2 127.2 %all-gather.3.cloned.1.call-start = ((), (), s32[]{:S(2)}) async-start(), calls=%async_computation.2 | async-start | bytes 1310720 | tf_op jit(solution)/shard_map/all_gather | solution.py:79
Sparse Core Ops, SparseCore 0:
  55.4 53.8 reduce-scatter.1
  111.4 27.9 all-gather.2
where the time goes:
time: 215 us; the launch traced here: 214 us
  other arithmetic  102 us (47%)
  waiting for transfers between devices  52.4 us (24%)
  local copies, waits for them, and re-layouts  16.8 us (8%)
  between operations  16.1 us (7%)
  matrix products  14.6 us (7%)
  blocking collectives  12.3 us (6%)
    convert_element_type x2, other arithmetic, phase_table(): (jnp.cos(angles) * factor).astype(jnp.bfloat16)  80.4 us
    reduce_scatter x1, waiting for transfers between devices, local(): lax.psum_scatter(jnp.stack([part_real.reshape(1 * lax.axis_size('col'), F...  52.3 us
    dot_general x2, matrix products, complex_product(): product = jnp.dot(left_rows, right_cols, preferred_element_type=jnp.float32)  14.6 us
    reshape x2, local copies, waits for them, and re-layouts, complex_product(): product = product.reshape(2, left_real.shape[0], 2, right_real.shape[1])  12.6 us
    pmax x1, blocking collectives, local(): peak = lax.pmax(local_peak[None], 'row')  12.3 us
    sub x2, other arithmetic, complex_product(): real_part = product[0, :, 0] - product[1, :, 1]  11.1 us
  transfers between devices with their start and end apart: 2, of which 1 were waited for; matrix products, arithmetic and copies ran while one was open for 34% of the time, Pallas kernels for 0%

commit v1 on v0

v1 whole, which is shorter than its diff:
```python
import functools
import math

import jax
import jax.numpy as jnp
from jax import lax
from jax.experimental import pallas as pl
from jax.experimental.pallas import tpu as pltpu
from jax.sharding import PartitionSpec as P

FS = 4096
NG = 16384
FR = 64
TWO_PI = 2.0 * math.pi
BEAM_SLOPE = 0.66
FINE = 32
CHUNKS = 4
MESH = pl.DeviceIdType.MESH
F32 = jnp.float32
BF16 = jnp.bfloat16


def cis(product):
    shift = (NG // 4).bit_length() - 1
    turn = product & (NG - 1)
    quadrant = (turn + NG // 8) >> shift
    rest = turn - (quadrant << shift)
    angle = rest.astype(F32) * (TWO_PI / NG)
    z = angle * angle
    sine = angle * (1.0 + z * (-1.0 / 6 + z * (1.0 / 120 + z * (-1.0 / 5040 + z * (1.0 / 362880)))))
    cosine = 1.0 + z * (-0.5 + z * (1.0 / 24 + z * (-1.0 / 720 + z * (1.0 / 40320))))
    odd = (quadrant & 1) == 1
    real = jnp.where(odd, sine, cosine)
    imag = jnp.where(odd, cosine, sine)
    real = jnp.where(((quadrant + 1) & 2) != 0, -real, real)
    imag = jnp.where((quadrant & 2) != 0, -imag, imag)
    return real, imag


def iota(shape, dim):
    return lax.broadcasted_iota(jnp.int32, shape, dim)


def kernel(
    cols, rows,
    vis_hbm, col_off, row_off, facet_off, facet_order, counts,
    image, peak,
    vis, head, fine, table, mine, pair_out, pair_in, sums, others, gathered,
    coarse2, fine2, table2, totals, peaks,
    vis_sem, pair_send, pair_recv, col_send, col_recv, row_send, row_recv, peak_send, peak_recv,
):
    m = vis.shape[1]
    width = m // CHUNKS
    chips = cols // 2
    block_cols = FS // rows
    me_col = lax.axis_index("col")
    me_row = lax.axis_index("row")
    core = lax.rem(me_col, 2)
    chip = me_col // 2
    partner = chip * 2 + 1 - core

    def peer_chip(d):
        return lax.rem(chip + d, chips) * 2 + core

    def peer_row(d):
        return lax.rem(me_row + d, rows)

    barrier = pltpu.get_barrier_semaphore()
    pl.semaphore_signal(barrier, inc=1, device_id=(partner, me_row), device_id_type=MESH)
    for d in range(1, chips):
        pl.semaphore_signal(barrier, inc=1, device_id=(peer_chip(d), me_row), device_id_type=MESH)
    for d in range(1, rows):
        pl.semaphore_signal(barrier, inc=1, device_id=(me_col, peer_row(d)), device_id_type=MESH)

    def vis_copy(k):
        part = pl.ds(k * width, width)
        return pltpu.make_async_copy(vis_hbm.at[:, :, part], vis.at[:, :, part], vis_sem.at[k])

    for k in range(CHUNKS):
        vis_copy(k).start()

    u = iota((cols, m), 1)
    slot = iota((cols, m), 0)
    start = jnp.zeros((cols, m), jnp.int32)
    for half in range(2):
        for c in range(chips):
            facet = facet_order[c * 2 + (core if half == 0 else 1 - core)]
            first = (facet_off[facet, 0] + (FS // 2 - FR // 2)) & (NG - 1)
            start = jnp.where(slot == half * chips + c, first, start)
    real, imag = cis(start * (col_off[0] + u))
    scale = jnp.where(u < counts[0, 0], 1.0 / math.sqrt(m * cols), 0.0)
    head[0] = real * scale
    head[1] = imag * scale
    real, imag = cis(iota((FR, m), 0) * (col_off[0] + iota((FR, m), 1)))
    fine[0] = real
    fine[1] = imag
    for s in range(cols):
        a, b = head[0, pl.ds(s, 1), :], head[1, pl.ds(s, 1), :]
        c, d = fine[0], fine[1]
        out = pl.ds(s * FR, FR)
        imag = a * d + b * c
        table[0, out, :] = (a * c - b * d).astype(BF16)
        table[1, out, :] = imag.astype(BF16)
        table[2, out, :] = (-imag).astype(BF16)

    pl.semaphore_wait(barrier, chips + rows - 1)

    def pair_copy(k):
        return pltpu.make_async_remote_copy(
            src_ref=pair_out.at[k], dst_ref=pair_in.at[k],
            send_sem=pair_send.at[k], recv_sem=pair_recv.at[k],
            device_id=(partner, me_row), device_id_type=MESH)

    def col_copy(k, d):
        target = lax.rem(chip + d, chips)
        return pltpu.make_async_remote_copy(
            src_ref=sums.at[k, target], dst_ref=others.at[k, d - 1],
            send_sem=col_send.at[k, d - 1], recv_sem=col_recv.at[k, d - 1],
            device_id=(target * 2 + core, me_row), device_id_type=MESH)

    def row_copy(k, origin, step):
        side = 0 if step > 0 else 1
        return pltpu.make_async_remote_copy(
            src_ref=gathered.at[k, origin], dst_ref=gathered.at[k, origin],
            send_sem=row_send.at[k, side, origin], recv_sem=row_recv.at[k, origin],
            device_id=(me_col, me_row + step), device_id_type=MESH)

    def transform(k):
        vis_copy(k).wait()
        part = pl.ds(k * width, width)
        vr, vi = vis[0, :, part], vis[1, :, part]
        dot = functools.partial(jnp.dot, preferred_element_type=F32)
        for half in (1, 0):
            own = pl.ds(half * chips * FR, chips * FR)
            tr, ti, tn = table[0, own, :], table[1, own, :], table[2, own, :]
            pr = (dot(tr, vr) + dot(tn, vi)).reshape(chips, FR, width)
            pi = (dot(tr, vi) + dot(ti, vr)).reshape(chips, FR, width)
            if half == 1:
                pair_out[k, :, pl.ds(0, FR), :] = pr.astype(BF16)
                pair_out[k, :, pl.ds(FR, FR), :] = pi.astype(BF16)
                pair_copy(k).start()
            else:
                mine[k, :, pl.ds(0, FR), :] = pr
                mine[k, :, pl.ds(FR, FR), :] = pi

    def pair_sum(k):
        pair_copy(k).wait_recv()
        sums[k] = (mine[k] + pair_in[k].astype(F32)).astype(BF16)
        for d in range(1, chips):
            col_copy(k, d).start()

    def facet_sum(k):
        total = mine[k, chip] + pair_in[k, chip].astype(F32)
        for d in range(1, chips):
            col_copy(k, d).wait_recv()
            total = total + others[k, d - 1].astype(F32)
        gathered[k, me_row] = total.astype(BF16)

        @pl.when(me_row < rows - 1)
        def _():
            row_copy(k, me_row, 1).start()

        @pl.when(me_row > 0)
        def _():
            row_copy(k, me_row, -1).start()

    def relay(k, dist):
        @pl.when(me_row - dist >= 0)
        def _():
            row_copy(k, me_row - dist, 1).wait_recv()

            @pl.when(me_row < rows - 1)
            def _():
                row_copy(k, me_row - dist, 1).start()

        @pl.when(me_row + dist < rows)
        def _():
            row_copy(k, me_row + dist, -1).wait_recv()

            @pl.when(me_row > 0)
            def _():
                row_copy(k, me_row + dist, -1).start()

    def second(k):
        left = gathered[k].reshape(rows * 2 * FR, width)
        part = pl.ds(k * width, width)
        for side in range(2):
            product = jnp.dot(left, table2[side, part, :], preferred_element_type=F32)
            if k == 0:
                totals[side] = product
            else:
                totals[side] += product

    transform(0)
    for k in range(1, CHUNKS):
        transform(k)
        pair_sum(k - 1)
    pair_sum(CHUNKS - 1)

    own_facet = facet_order[me_col]
    column0 = (facet_off[own_facet, 1] + me_row * block_cols) & (NG - 1)
    shape = (m // FINE, block_cols)
    real, imag = cis(iota(shape, 0) * FINE * (column0 + iota(shape, 1)))
    coarse2[0] = real
    coarse2[1] = imag
    shape = (FINE, block_cols)
    real, imag = cis(iota(shape, 0) * (column0 + iota(shape, 1)))
    fine2[0] = real
    fine2[1] = imag

    def row_table(h, carry):
        a, b = coarse2[0, pl.ds(h, 1), :], coarse2[1, pl.ds(h, 1), :]
        c, d = fine2[0], fine2[1]
        out = pl.ds(pl.multiple_of(h * FINE, FINE), FINE)
        table2[0, out, :] = (a * c - b * d).astype(BF16)
        table2[1, out, :] = (a * d + b * c).astype(BF16)
        return carry

    lax.fori_loop(0, m // FINE, row_table, 0)

    row_ids = iota((rows, block_cols), 0)
    offsets = jnp.zeros((rows, block_cols), jnp.int32)
    for r in range(rows):
        offsets = jnp.where(row_ids == r, row_off[r], offsets)
    lanes = iota((rows, block_cols), 1)
    beam = 1.0 - BEAM_SLOPE * ((me_row * block_cols + lanes).astype(F32) + 0.5) / FS
    gain = (0.5 / math.sqrt(m * rows)) / beam
    phase_real, phase_imag = cis(offsets * ((column0 + lanes) & (NG - 1)))
    phase_real, phase_imag = phase_real * gain, phase_imag * gain

    for step in range(CHUNKS + rows - 1):
        if step < CHUNKS:
            facet_sum(step)
        for dist in range(1, rows):
            k = step - dist
            if 0 <= k < CHUNKS:
                relay(k, dist)
                if dist == rows - 1:
                    second(k)

    out_real = jnp.zeros((FR, block_cols), F32)
    out_imag = jnp.zeros((FR, block_cols), F32)
    for r in range(rows):
        top, low = pl.ds(r * 2 * FR, FR), pl.ds(r * 2 * FR + FR, FR)
        real = totals[0, top, :] - totals[1, low, :]
        imag = totals[1, top, :] + totals[0, low, :]
        a, b = phase_real[r : r + 1], phase_imag[r : r + 1]
        out_real = out_real + (real * a - imag * b)
        out_imag = out_imag + (real * b + imag * a)
    image[0, 0] = out_real
    image[0, 1] = out_imag
    power = out_real * out_real + out_imag * out_imag
    power = jnp.max(power.reshape(FR // 8, 8, block_cols), axis=0)
    best = power[:, :128]
    for n in range(1, block_cols // 128):
        best = jnp.maximum(best, power[:, n * 128 : (n + 1) * 128])
    peaks[me_row] = jnp.sqrt(best)

    def peak_copy(d):
        return pltpu.make_async_remote_copy(
            src_ref=peaks.at[me_row], dst_ref=peaks.at[me_row],
            send_sem=peak_send.at[d - 1], recv_sem=peak_recv.at[d - 1],
            device_id=(me_col, peer_row(d)), device_id_type=MESH)

    for d in range(1, rows):
        peak_copy(d).start()

    for k in range(CHUNKS):
        pair_copy(k).wait_send()
        for d in range(1, chips):
            col_copy(k, d).wait_send()

        @pl.when(me_row < rows - 1)
        def _():
            row_copy(k, me_row, 1).wait_send()

        @pl.when(me_row > 0)
        def _():
            row_copy(k, me_row, -1).wait_send()

        for dist in range(1, rows):
            @pl.when((me_row - dist >= 0) & (me_row < rows - 1))
            def _():
                row_copy(k, me_row - dist, 1).wait_send()

            @pl.when((me_row + dist < rows) & (me_row > 0))
            def _():
                row_copy(k, me_row + dist, -1).wait_send()

    for d in range(1, rows):
        peak_copy(d).wait()
    best = peaks[0]
    for r in range(1, rows):
        best = jnp.maximum(best, peaks[r])
    peak[0] = jnp.max(best)


def local(cols, rows, visibilities, col_offsets, row_offsets, facet_offsets, facet_order, vis_counts):
    m = visibilities.shape[1]
    width = m // CHUNKS
    chips = cols // 2
    block_cols = FS // rows
    dma = pltpu.SemaphoreType.DMA
    smem = pl.BlockSpec(memory_space=pltpu.SMEM)
    return pl.pallas_call(
        functools.partial(kernel, cols, rows),
        out_shape=(
            jax.ShapeDtypeStruct((1, 2, FR, block_cols), F32),
            jax.ShapeDtypeStruct((1,), F32),
        ),
        in_specs=[pl.BlockSpec(memory_space=pl.ANY)] + [smem] * 5,
        out_specs=(pl.BlockSpec(memory_space=pltpu.VMEM), smem),
        scratch_shapes=[
            pltpu.VMEM((2, m, m), BF16),
            pltpu.VMEM((2, cols, m), F32),
            pltpu.VMEM((2, FR, m), F32),
            pltpu.VMEM((3, cols * FR, m), BF16),
            pltpu.VMEM((CHUNKS, chips, 2 * FR, width), F32),
            pltpu.VMEM((CHUNKS, chips, 2 * FR, width), BF16),
            pltpu.VMEM((CHUNKS, chips, 2 * FR, width), BF16),
            pltpu.VMEM((CHUNKS, chips, 2 * FR, width), BF16),
            pltpu.VMEM((CHUNKS, chips - 1, 2 * FR, width), BF16),
            pltpu.VMEM((CHUNKS, rows, 2 * FR, width), BF16),
            pltpu.VMEM((2, m // FINE, block_cols), F32),
            pltpu.VMEM((2, FINE, block_cols), F32),
            pltpu.VMEM((2, m, block_cols), BF16),
            pltpu.VMEM((2, rows * 2 * FR, block_cols), F32),
            pltpu.VMEM((rows, 8, 128), F32),
            dma((CHUNKS,)),
            dma((CHUNKS,)),
            dma((CHUNKS,)),
            dma((CHUNKS, chips - 1)),
            dma((CHUNKS, chips - 1)),
            dma((CHUNKS, 2, rows)),
            dma((CHUNKS, rows)),
            dma((rows - 1,)),
            dma((rows - 1,)),
        ],
        compiler_params=pltpu.CompilerParams(
            collective_id=0, has_side_effects=True, vmem_limit_bytes=60 * 1024 * 1024),
    )(visibilities, col_offsets, row_offsets, facet_offsets, facet_order, vis_counts)


def solution(mesh):
    in_specs = (P(None, "col", "row"), P("col"), P(), P(), P(), P("col", "row"))
    out_specs = (P("col", None, None, "row"), P("col"))
    body = functools.partial(local, mesh.shape["col"], mesh.shape["row"])
    return jax.shard_map(body, mesh=mesh, in_specs=in_specs, out_specs=out_specs, check_vma=False)
```

time: 215 us -> 46.3 us (0.22)
  other arithmetic: 102 us -> 0 us
  waiting for transfers between devices: 52.4 us -> 0 us
  Pallas kernels: 0 us -> 39.2 us
  matrix products: 14.6 us -> 0 us
  local copies, waits for them, and re-layouts: 16.8 us -> 3.23 us
  between operations: 16.1 us -> 3.63 us
  blocking collectives: 12.3 us -> 0 us
    convert_element_type x5 -> x0, other arithmetic: 82.9 us -> none  [the longest x2 80.4 us: phase_table(): (jnp.cos(angles) * factor).astype(jnp.bfloat16)]
    reduce_scatter x1 -> x0, waiting for transfers between devices: 52.3 us -> none  [local(): lax.psum_scatter(jnp.stack([part_real.reshape(1 * lax.axis_size('col'), F...]
    pallas_call x0 -> x1, Pallas kernels: none -> 39.2 us  [local(): pl.pallas_call(functools.partial(kernel, cols, rows), out_shape=(jax.Shap...]
    dot_general x2 -> x0, matrix products: 14.6 us -> none  [complex_product(): product = jnp.dot(left_rows, right_cols, preferred_element_type=jnp.float32)]
    reshape x2 -> x0, local copies, waits for them, and re-layouts: 12.6 us -> none  [complex_product(): product = product.reshape(2, left_real.shape[0], 2, right_real.shape[1])]
    pmax x1 -> x0, blocking collectives: 12.3 us -> none  [local(): peak = lax.pmax(local_peak[None], 'row')]
    sub x3 -> x0, other arithmetic: 11.1 us -> none  [the longest x2 11.1 us: complex_product(): real_part = product[0, :, 0] - product[1, :, 1]]
    select_n x3 -> x0, other arithmetic: 2.57 us -> none  [the longest x1 2.54 us: local(): jnp.where(live_rows[None, :, None], visibilities, jnp.zeros_like(visibili...]
  transfers between devices with their start and end apart: 2 -> 0, of which waited for: 1 -> 0; matrix products, arithmetic and copies ran while one was open for 34% -> 0% of each run, Pallas kernels for 0% -> 0%
where the time goes in v1:
time: 46.3 us; the launch traced here: 46 us
  Pallas kernels  39.2 us (85%)
  between operations  3.63 us (8%)
  local copies, waits for them, and re-layouts  3.23 us (7%)
    pallas_call x1, Pallas kernels, local(): pl.pallas_call(functools.partial(kernel, cols, rows), out_shape=(jax.Shap...  39.2 us
    unnamed x2, local copies, waits for them, and re-layouts  3.23 us

profile of v1, /device:TPU:0, one launch (start us, length us, event | category | flops | bytes accessed | tf_op | source)
XLA Modules:
  0.0 46.0 jit_solution(14771615859446637222)
XLA Ops:
  1.9 1.3 %copy.8.facet_off = s32[8,2]{1,0:T(8,128)} copy(s32[8,2]{0,1:T(2,128)} %param.9) | data formatting | bytes 128 | tf_op args[3]
  3.3 39.2 %shard_map.77 = (f32[1,2,64,1024]{3,2,1,0:T(8,128)}, f32[1]{0:T(128)}) custom-call(bf16[2,1024,1024]{2,1,0:T(8,128)(2,1)} %vis_hbm.1, s32[1]{0:T(128)S(6)} %copy.11.col_off, s32[4]{0:T(128)} %row_off.1, s32[8,2]{1,0:T(8,128)} %copy.8.facet_off, s32[8]{0:T(128)} %facet_order.1, s32[1,1]{1,0:T(1,128)S(6)} %copy.12.counts), custom_call_target="tpu_custom_call" | custom-call | tf_op jit(solution)/shard_map/pallas_call | solution.py:305
  42.5 1.9 %copy.13 = f32[1,2,64,1024]{3,2,1,0:T(8,128)} copy(f32[1,2,64,1024]{3,2,1,0:T(8,128)} %get-tuple-element.4) | data formatting | bytes 1048576

commit v2 on v1

--- a/solution.py
+++ b/solution.py
@@ -43,12 +43,21 @@
 
 def kernel(
     cols, rows,
-    vis_hbm, col_off, row_off, facet_off, facet_order, counts,
-    image, peak,
+    vis_hbm, *refs,
+):
+    small, (image, peak), scratch = refs[:5], refs[5:7], refs[7:]
+    (
+    col_off, row_off, facet_off, facet_order, counts, small_sem,
     vis, head, fine, table, mine, pair_out, pair_in, sums, others, gathered,
     coarse2, fine2, table2, totals, peaks,
     vis_sem, pair_send, pair_recv, col_send, col_recv, row_send, row_recv, peak_send, peak_recv,
-):
+    ) = scratch
+    copies = [
+        pltpu.make_async_copy(source, target, small_sem.at[n])
+        for n, (source, target) in enumerate(zip(small, scratch[:5]))
+    ]
+    for copy in copies:
+        copy.start()
     m = vis.shape[1]
     width = m // CHUNKS
     chips = cols // 2
@@ -79,13 +88,16 @@
     for k in range(CHUNKS):
         vis_copy(k).start()
 
+    for copy in copies:
+        copy.wait()
+
     u = iota((cols, m), 1)
     slot = iota((cols, m), 0)
     start = jnp.zeros((cols, m), jnp.int32)
     for half in range(2):
         for c in range(chips):
             facet = facet_order[c * 2 + (core if half == 0 else 1 - core)]
-            first = (facet_off[facet, 0] + (FS // 2 - FR // 2)) & (NG - 1)
+            first = (facet_off[0, facet] + (FS // 2 - FR // 2)) & (NG - 1)
             start = jnp.where(slot == half * chips + c, first, start)
     real, imag = cis(start * (col_off[0] + u))
     scale = jnp.where(u < counts[0, 0], 1.0 / math.sqrt(m * cols), 0.0)
@@ -97,11 +109,11 @@
     for s in range(cols):
         a, b = head[0, pl.ds(s, 1), :], head[1, pl.ds(s, 1), :]
         c, d = fine[0], fine[1]
-        out = pl.ds(s * FR, FR)
+        half, block, at = s // chips, chips * FR, s % chips * FR
         imag = a * d + b * c
-        table[0, out, :] = (a * c - b * d).astype(BF16)
-        table[1, out, :] = imag.astype(BF16)
-        table[2, out, :] = (-imag).astype(BF16)
+        table[half, pl.ds(at, FR), :] = (-imag).astype(BF16)
+        table[half, pl.ds(block + at, FR), :] = (a * c - b * d).astype(BF16)
+        table[half, pl.ds(2 * block + at, FR), :] = imag.astype(BF16)
 
     pl.semaphore_wait(barrier, chips + rows - 1)
 
@@ -125,23 +137,23 @@
             send_sem=row_send.at[k, side, origin], recv_sem=row_recv.at[k, origin],
             device_id=(me_col, me_row + step), device_id_type=MESH)
 
-    def transform(k):
-        vis_copy(k).wait()
+    def transform(k, half):
+        if half == 1:
+            vis_copy(k).wait()
         part = pl.ds(k * width, width)
-        vr, vi = vis[0, :, part], vis[1, :, part]
+        block = chips * FR
         dot = functools.partial(jnp.dot, preferred_element_type=F32)
-        for half in (1, 0):
-            own = pl.ds(half * chips * FR, chips * FR)
-            tr, ti, tn = table[0, own, :], table[1, own, :], table[2, own, :]
-            pr = (dot(tr, vr) + dot(tn, vi)).reshape(chips, FR, width)
-            pi = (dot(tr, vi) + dot(ti, vr)).reshape(chips, FR, width)
-            if half == 1:
-                pair_out[k, :, pl.ds(0, FR), :] = pr.astype(BF16)
-                pair_out[k, :, pl.ds(FR, FR), :] = pi.astype(BF16)
-                pair_copy(k).start()
-            else:
-                mine[k, :, pl.ds(0, FR), :] = pr
-                mine[k, :, pl.ds(FR, FR), :] = pi
+        both = dot(table[half, pl.ds(block, 2 * block), :], vis[0, :, part])
+        both += dot(table[half, pl.ds(0, 2 * block), :], vis[1, :, part])
+        pr = both[:block].reshape(chips, FR, width)
+        pi = both[block:].reshape(chips, FR, width)
+        if half == 1:
+            pair_out[k, :, pl.ds(0, FR), :] = pr.astype(BF16)
+            pair_out[k, :, pl.ds(FR, FR), :] = pi.astype(BF16)
+            pair_copy(k).start()
+        else:
+            mine[k, :, pl.ds(0, FR), :] = pr
+            mine[k, :, pl.ds(FR, FR), :] = pi
 
     def pair_sum(k):
         pair_copy(k).wait_recv()
@@ -191,14 +203,17 @@
             else:
                 totals[side] += product
 
-    transform(0)
+    transform(0, 1)
+    transform(0, 0)
     for k in range(1, CHUNKS):
-        transform(k)
+        transform(k, 1)
         pair_sum(k - 1)
+        transform(k, 0)
     pair_sum(CHUNKS - 1)
+    facet_sum(0)
 
     own_facet = facet_order[me_col]
-    column0 = (facet_off[own_facet, 1] + me_row * block_cols) & (NG - 1)
+    column0 = (facet_off[1, own_facet] + me_row * block_cols) & (NG - 1)
     shape = (m // FINE, block_cols)
     real, imag = cis(iota(shape, 0) * FINE * (column0 + iota(shape, 1)))
     coarse2[0] = real
@@ -229,7 +244,7 @@
     phase_real, phase_imag = phase_real * gain, phase_imag * gain
 
     for step in range(CHUNKS + rows - 1):
-        if step < CHUNKS:
+        if 0 < step < CHUNKS:
             facet_sum(step)
         for dist in range(1, rows):
             k = step - dist
@@ -302,19 +317,22 @@
     block_cols = FS // rows
     dma = pltpu.SemaphoreType.DMA
     smem = pl.BlockSpec(memory_space=pltpu.SMEM)
+    anywhere = pl.BlockSpec(memory_space=pl.ANY)
+    small = (col_offsets, row_offsets, facet_offsets.T, facet_order, vis_counts)
     return pl.pallas_call(
         functools.partial(kernel, cols, rows),
         out_shape=(
-            jax.ShapeDtypeStruct((1, 2, FR, block_cols), F32),
+            pltpu.VMEM((1, 2, FR, block_cols), F32),
             jax.ShapeDtypeStruct((1,), F32),
         ),
-        in_specs=[pl.BlockSpec(memory_space=pl.ANY)] + [smem] * 5,
+        in_specs=[anywhere] * 6,
         out_specs=(pl.BlockSpec(memory_space=pltpu.VMEM), smem),
-        scratch_shapes=[
+        scratch_shapes=[pltpu.SMEM(x.shape, x.dtype) for x in small] + [
+            dma((len(small),)),
             pltpu.VMEM((2, m, m), BF16),
             pltpu.VMEM((2, cols, m), F32),
             pltpu.VMEM((2, FR, m), F32),
-            pltpu.VMEM((3, cols * FR, m), BF16),
+            pltpu.VMEM((2, 3 * chips * FR, m), BF16),
             pltpu.VMEM((CHUNKS, chips, 2 * FR, width), F32),
             pltpu.VMEM((CHUNKS, chips, 2 * FR, width), BF16),
             pltpu.VMEM((CHUNKS, chips, 2 * FR, width), BF16),
@@ -338,7 +356,7 @@
         ],
         compiler_params=pltpu.CompilerParams(
             collective_id=0, has_side_effects=True, vmem_limit_bytes=60 * 1024 * 1024),
-    )(visibilities, col_offsets, row_offsets, facet_offsets, facet_order, vis_counts)
+    )(visibilities, *small)
 
 
 def solution(mesh):

time: 46.3 us -> 45.3 us (0.978)
  local copies, waits for them, and re-layouts: 3.23 us -> 0.8 us
  Pallas kernels: 39.2 us -> 40.7 us
    unnamed x2 -> x1, local copies, waits for them, and re-layouts: 3.23 us -> 0.8 us
    pallas_call x1, Pallas kernels: 39.2 us -> 40.7 us  [local(): pl.pallas_call(functools.partial(kernel, cols, rows), out_shape=(pltpu.VM...]
where the time goes in v2:
time: 45.3 us; the launch traced here: 45.1 us
  Pallas kernels  40.7 us (90%)
  between operations  3.62 us (8%)
  local copies, waits for them, and re-layouts  0.8 us (2%)
    pallas_call x1, Pallas kernels, local(): pl.pallas_call(functools.partial(kernel, cols, rows), out_shape=(pltpu.VM...  40.7 us

profile of v2, /device:TPU:0, one launch (start us, length us, event | category | flops | bytes accessed | tf_op | source)
XLA Modules:
  0.0 45.1 jit_solution(16559585920893148010)
XLA Ops:
  1.9 40.7 %shard_map.77 = (f32[1,2,64,1024]{3,2,1,0:T(8,128)S(1)}, f32[1]{0:T(128)}) custom-call(bf16[2,1024,1024]{2,1,0:T(8,128)(2,1)} %vis_hbm.1, s32[1]{0:T(128)S(6)} %copy.11.refs_0_, s32[4]{0:T(128)} %refs_1_.1, s32[2,8]{1,0:T(2,128)} %bitcast.1, s32[8]{0:T(128)} %refs_3_.1, s32[1,1]{1,0:T(1,128)S(6)} %copy.12.refs_4_), custom_call_target="tpu_custom_call" | custom-call | tf_op jit(solution)/shard_map/pallas_call | solution.py:322
  42.6 0.8 %copy.10 = f32[1,2,64,1024]{3,2,1,0:T(8,128)} copy(f32[1,2,64,1024]{3,2,1,0:T(8,128)S(1)} %get-tuple-element.2) | data formatting | bytes 1048576

commit v3 on v2

--- a/solution.py
+++ b/solution.py
@@ -14,7 +14,9 @@
 TWO_PI = 2.0 * math.pi
 BEAM_SLOPE = 0.66
 FINE = 32
-CHUNKS = 4
+CHUNKS = 8
+GROUPS = 4
+WIDE = CHUNKS // GROUPS
 MESH = pl.DeviceIdType.MESH
 F32 = jnp.float32
 BF16 = jnp.bfloat16
@@ -82,11 +84,11 @@
         pl.semaphore_signal(barrier, inc=1, device_id=(me_col, peer_row(d)), device_id_type=MESH)
 
     def vis_copy(k):
-        part = pl.ds(k * width, width)
+        part = pl.ds(k * WIDE * width, WIDE * width)
         return pltpu.make_async_copy(vis_hbm.at[:, :, part], vis.at[:, :, part], vis_sem.at[k])
 
-    for k in range(CHUNKS):
-        vis_copy(k).start()
+    for g in range(GROUPS):
+        vis_copy(g).start()
 
     for copy in copies:
         copy.wait()
@@ -106,16 +108,16 @@
     real, imag = cis(iota((FR, m), 0) * (col_off[0] + iota((FR, m), 1)))
     fine[0] = real
     fine[1] = imag
-    for s in range(cols):
-        a, b = head[0, pl.ds(s, 1), :], head[1, pl.ds(s, 1), :]
-        c, d = fine[0], fine[1]
-        half, block, at = s // chips, chips * FR, s % chips * FR
-        imag = a * d + b * c
-        table[half, pl.ds(at, FR), :] = (-imag).astype(BF16)
-        table[half, pl.ds(block + at, FR), :] = (a * c - b * d).astype(BF16)
-        table[half, pl.ds(2 * block + at, FR), :] = imag.astype(BF16)
-
-    pl.semaphore_wait(barrier, chips + rows - 1)
+    def column_table(half):
+        block = chips * FR
+        for at in range(chips):
+            s = half * chips + at
+            a, b = head[0, pl.ds(s, 1), :], head[1, pl.ds(s, 1), :]
+            c, d = fine[0], fine[1]
+            imag = a * d + b * c
+            table[half, pl.ds(at * FR, FR), :] = (-imag).astype(BF16)
+            table[half, pl.ds(block + at * FR, FR), :] = (a * c - b * d).astype(BF16)
+            table[half, pl.ds(2 * block + at * FR, FR), :] = imag.astype(BF16)
 
     def pair_copy(k):
         return pltpu.make_async_remote_copy(
@@ -137,23 +139,26 @@
             send_sem=row_send.at[k, side, origin], recv_sem=row_recv.at[k, origin],
             device_id=(me_col, me_row + step), device_id_type=MESH)
 
-    def transform(k, half):
-        if half == 1:
-            vis_copy(k).wait()
-        part = pl.ds(k * width, width)
+    def transform(first, count, half):
+        part = pl.ds(first * width, count * width)
         block = chips * FR
         dot = functools.partial(jnp.dot, preferred_element_type=F32)
         both = dot(table[half, pl.ds(block, 2 * block), :], vis[0, :, part])
         both += dot(table[half, pl.ds(0, 2 * block), :], vis[1, :, part])
-        pr = both[:block].reshape(chips, FR, width)
-        pi = both[block:].reshape(chips, FR, width)
-        if half == 1:
-            pair_out[k, :, pl.ds(0, FR), :] = pr.astype(BF16)
-            pair_out[k, :, pl.ds(FR, FR), :] = pi.astype(BF16)
-            pair_copy(k).start()
-        else:
-            mine[k, :, pl.ds(0, FR), :] = pr
-            mine[k, :, pl.ds(FR, FR), :] = pi
+        for n in range(count):
+            k = first + n
+            piece = both[:, n * width : (n + 1) * width]
+            pr = piece[:block].reshape(chips, FR, width)
+            pi = piece[block:].reshape(chips, FR, width)
+            if half == 1:
+                pair_out[k, :, pl.ds(0, FR), :] = pr.astype(BF16)
+                pair_out[k, :, pl.ds(FR, FR), :] = pi.astype(BF16)
+                if k == 0:
+                    pl.semaphore_wait(barrier, chips + rows - 1)
+                pair_copy(k).start()
+            else:
+                mine[k, :, pl.ds(0, FR), :] = pr
+                mine[k, :, pl.ds(FR, FR), :] = pi
 
     def pair_sum(k):
         pair_copy(k).wait_recv()
@@ -193,24 +198,39 @@
             def _():
                 row_copy(k, me_row + dist, -1).start()
 
-    def second(k):
-        left = gathered[k].reshape(rows * 2 * FR, width)
-        part = pl.ds(k * width, width)
+    def second(g):
+        left = jnp.concatenate(
+            [gathered[g * WIDE + n].reshape(rows * 2 * FR, width) for n in range(WIDE)], axis=1)
+        part = pl.ds(g * WIDE * width, WIDE * width)
         for side in range(2):
             product = jnp.dot(left, table2[side, part, :], preferred_element_type=F32)
-            if k == 0:
+            if g == 0:
                 totals[side] = product
             else:
                 totals[side] += product
 
-    transform(0, 1)
-    transform(0, 0)
-    for k in range(1, CHUNKS):
-        transform(k, 1)
-        pair_sum(k - 1)
-        transform(k, 0)
-    pair_sum(CHUNKS - 1)
-    facet_sum(0)
+    vis_copy(0).wait()
+    column_table(1)
+    transform(0, 1, 1)
+    column_table(0)
+    transform(0, 1, 0)
+    transform(1, 1, 1)
+    pair_sum(0)
+    transform(1, 1, 0)
+    for g in range(1, GROUPS):
+        vis_copy(g).wait()
+        transform(g * WIDE, WIDE, 1)
+        if g == 1:
+            pair_sum(1)
+        else:
+            for n in range(WIDE):
+                pair_sum((g - 1) * WIDE + n)
+        if g == GROUPS - 1:
+            facet_sum(0)
+        transform(g * WIDE, WIDE, 0)
+    for n in range(WIDE):
+        pair_sum((GROUPS - 1) * WIDE + n)
+    facet_sum(1)
 
     own_facet = facet_order[me_col]
     column0 = (facet_off[1, own_facet] + me_row * block_cols) & (NG - 1)
@@ -244,14 +264,14 @@
     phase_real, phase_imag = phase_real * gain, phase_imag * gain
 
     for step in range(CHUNKS + rows - 1):
-        if 0 < step < CHUNKS:
+        if 1 < step < CHUNKS:
             facet_sum(step)
         for dist in range(1, rows):
             k = step - dist
             if 0 <= k < CHUNKS:
                 relay(k, dist)
-                if dist == rows - 1:
-                    second(k)
+                if dist == rows - 1 and k % WIDE == WIDE - 1:
+                    second(k // WIDE)
 
     out_real = jnp.zeros((FR, block_cols), F32)
     out_imag = jnp.zeros((FR, block_cols), F32)
@@ -344,7 +364,7 @@
             pltpu.VMEM((2, m, block_cols), BF16),
             pltpu.VMEM((2, rows * 2 * FR, block_cols), F32),
             pltpu.VMEM((rows, 8, 128), F32),
-            dma((CHUNKS,)),
+            dma((GROUPS,)),
             dma((CHUNKS,)),
             dma((CHUNKS,)),
             dma((CHUNKS, chips - 1)),

time: 45.3 us -> 51.6 us (1.14)
  Pallas kernels: 40.7 us -> 47 us
    pallas_call x1, Pallas kernels: 40.7 us -> 47 us  [local(): pl.pallas_call(functools.partial(kernel, cols, rows), out_shape=(pltpu.VM...]
where the time goes in v3:
time: 51.6 us; the launch traced here: 51.4 us
  Pallas kernels  47 us (91%)
  between operations  3.62 us (7%)
  local copies, waits for them, and re-layouts  0.8 us (2%)
    pallas_call x1, Pallas kernels, local(): pl.pallas_call(functools.partial(kernel, cols, rows), out_shape=(pltpu.VM...  47 us

profile of v3, /device:TPU:0, one launch (start us, length us, event | category | flops | bytes accessed | tf_op | source)
XLA Modules:
  0.0 51.4 jit_solution(9712271956876130719)
XLA Ops:
  1.9 47.0 %shard_map.77 = (f32[1,2,64,1024]{3,2,1,0:T(8,128)S(1)}, f32[1]{0:T(128)}) custom-call(bf16[2,1024,1024]{2,1,0:T(8,128)(2,1)} %vis_hbm.1, s32[1]{0:T(128)S(6)} %copy.11.refs_0_, s32[4]{0:T(128)} %refs_1_.1, s32[2,8]{1,0:T(2,128)} %bitcast.1, s32[8]{0:T(128)} %refs_3_.1, s32[1,1]{1,0:T(1,128)S(6)} %copy.12.refs_4_), custom_call_target="tpu_custom_call" | custom-call | tf_op jit(solution)/shard_map/pallas_call | solution.py:342
  48.9 0.8 %copy.10 = f32[1,2,64,1024]{3,2,1,0:T(8,128)} copy(f32[1,2,64,1024]{3,2,1,0:T(8,128)S(1)} %get-tuple-element.2) | data formatting | bytes 1048576

commit v4 on v2

--- a/solution.py
+++ b/solution.py
@@ -106,16 +106,16 @@
     real, imag = cis(iota((FR, m), 0) * (col_off[0] + iota((FR, m), 1)))
     fine[0] = real
     fine[1] = imag
-    for s in range(cols):
-        a, b = head[0, pl.ds(s, 1), :], head[1, pl.ds(s, 1), :]
-        c, d = fine[0], fine[1]
-        half, block, at = s // chips, chips * FR, s % chips * FR
-        imag = a * d + b * c
-        table[half, pl.ds(at, FR), :] = (-imag).astype(BF16)
-        table[half, pl.ds(block + at, FR), :] = (a * c - b * d).astype(BF16)
-        table[half, pl.ds(2 * block + at, FR), :] = imag.astype(BF16)
-
-    pl.semaphore_wait(barrier, chips + rows - 1)
+    def column_table(half):
+        block = chips * FR
+        for at in range(chips):
+            s = half * chips + at
+            a, b = head[0, pl.ds(s, 1), :], head[1, pl.ds(s, 1), :]
+            c, d = fine[0], fine[1]
+            imag = a * d + b * c
+            table[half, pl.ds(at * FR, FR), :] = (-imag).astype(BF16)
+            table[half, pl.ds(block + at * FR, FR), :] = (a * c - b * d).astype(BF16)
+            table[half, pl.ds(2 * block + at * FR, FR), :] = imag.astype(BF16)
 
     def pair_copy(k):
         return pltpu.make_async_remote_copy(
@@ -150,6 +150,8 @@
         if half == 1:
             pair_out[k, :, pl.ds(0, FR), :] = pr.astype(BF16)
             pair_out[k, :, pl.ds(FR, FR), :] = pi.astype(BF16)
+            if k == 0:
+                pl.semaphore_wait(barrier, chips + rows - 1)
             pair_copy(k).start()
         else:
             mine[k, :, pl.ds(0, FR), :] = pr
@@ -203,7 +205,9 @@
             else:
                 totals[side] += product
 
+    column_table(1)
     transform(0, 1)
+    column_table(0)
     transform(0, 0)
     for k in range(1, CHUNKS):
         transform(k, 1)

time: 45.3 us -> 44.4 us (0.980)
  Pallas kernels: 40.7 us -> 39.8 us
    pallas_call x1, Pallas kernels: 40.7 us -> 39.8 us  [local(): pl.pallas_call(functools.partial(kernel, cols, rows), out_shape=(pltpu.VM...]
where the time goes in v4:
time: 44.4 us; the launch traced here: 44.3 us
  Pallas kernels  39.8 us (90%)
  between operations  3.62 us (8%)
  local copies, waits for them, and re-layouts  0.8 us (2%)
    pallas_call x1, Pallas kernels, local(): pl.pallas_call(functools.partial(kernel, cols, rows), out_shape=(pltpu.VM...  39.8 us

profile of v4, /device:TPU:0, one launch (start us, length us, event | category | flops | bytes accessed | tf_op | source)
XLA Modules:
  0.0 44.3 jit_solution(5105515084579326576)
XLA Ops:
  1.9 39.8 %shard_map.77 = (f32[1,2,64,1024]{3,2,1,0:T(8,128)S(1)}, f32[1]{0:T(128)}) custom-call(bf16[2,1024,1024]{2,1,0:T(8,128)(2,1)} %vis_hbm.1, s32[1]{0:T(128)S(6)} %copy.11.refs_0_, s32[4]{0:T(128)} %refs_1_.1, s32[2,8]{1,0:T(2,128)} %bitcast.1, s32[8]{0:T(128)} %refs_3_.1, s32[1,1]{1,0:T(1,128)S(6)} %copy.12.refs_4_), custom_call_target="tpu_custom_call" | custom-call | tf_op jit(solution)/shard_map/pallas_call | solution.py:326
  41.8 0.8 %copy.10 = f32[1,2,64,1024]{3,2,1,0:T(8,128)} copy(f32[1,2,64,1024]{3,2,1,0:T(8,128)S(1)} %get-tuple-element.2) | data formatting | bytes 1048576
